TPU v7x, 32 devices: a whole 2x2x4 slice. The times are simulated.
32 devices in a mesh: gx: 8 (over z, x), gy: 4 (over y, core).
Axes of the slice: x: 2, y: 2, z: 4, core: 2. Of those that a mesh axis runs over, the one named last changes fastest.
Arguments:
- state: float32 [65536, 128], P(('gx', 'gy')), may hold values from 0 to 1
- velocity: bfloat16 [3, 3, 128, 64, 128], P(None, None, 'gx', 'gy'), may hold values from -3 to 3
- cells: int32 [3, 3, 65536], P(None, None, ('gx', 'gy')), may hold values from -1 to 126, as said below
- slots: int32 [3, 65536], P(None, ('gx', 'gy')), may hold values from 0 to 2047, as said below
- counts: int32 [3, 8, 4, 8], P(None, 'gx', 'gy'), may hold values from 0 to 64, as said below
Outputs:
- final_state: float32 [65536, 128], P(('gx', 'gy'))
Inputs may be any that keep to these rules, and one draw needn't show every extreme that they name: For every section and device the 2048 values of slots are a permutation of 0 to 2047. counts[s, i, j, r] equals counts[s, i', j', r xor 1] where (i', j') is the neighbour of (i, j) in direction r; some device sends exactly 64 in every section. cells[s, 0] lies in -1 to 15, cells[s, 1] in -1 to 15, cells[s, 2] in 0 to 126.
All inputs are finite; a program needn't handle non-finite values.
Results may differ from a plain program's by a relative error of at most 0.0003.
Values may be sent and summed in bfloat16 or wider, within the bound.
A program may use at most 64 MiB of HBM per device.

v0:
```python
import functools

import jax
import jax.numpy as jnp
from jax import lax
from jax.experimental import pallas as pl
from jax.experimental.pallas import tpu as pltpu
from jax.sharding import PartitionSpec as P

GAMMA = (8.0 / 15.0, 5.0 / 12.0, 3.0 / 4.0)
ZETA = (0.0, -17.0 / 60.0, -5.0 / 12.0)
OFFSETS = ((1, 0), (-1, 0), (0, 1), (0, -1), (1, 1), (-1, -1), (1, -1), (-1, 1))
SPARE = 8
MESH = pl.DeviceIdType.MESH
VMEM = pl.BlockSpec(memory_space=pltpu.VMEM)
SMEM = pl.BlockSpec(memory_space=pltpu.SMEM)


def neighbour(r, sizes):
    off_x, off_y = OFFSETS[r]
    i, j = lax.axis_index("gx"), lax.axis_index("gy")
    return (lax.rem(i + off_x + sizes[0], sizes[0]), lax.rem(j + off_y + sizes[1], sizes[1]))


def greet(sizes):
    barrier = pltpu.get_barrier_semaphore()
    for r in range(8):
        pl.semaphore_signal(barrier, inc=1, device_id=neighbour(r, sizes), device_id_type=MESH)
    pl.semaphore_wait(barrier, 8)


def send(r, src, dst, sems, group, sizes):
    copy = pltpu.make_async_remote_copy(
        src_ref=src,
        dst_ref=dst,
        send_sem=sems[0].at[group, r],
        recv_sem=sems[1].at[group, r ^ 1],
        device_id=neighbour(r, sizes),
        device_id_type=MESH,
    )
    copy.start()
    return copy


def parts_of(x):
    high = x.astype(jnp.bfloat16)
    rest = x - high.astype(jnp.float32)
    middle = rest.astype(jnp.bfloat16)
    low = (rest - middle.astype(jnp.float32)).astype(jnp.bfloat16)
    return high, middle, low


def cell_weights(size, cell, frac):
    spots = lax.broadcasted_iota(jnp.int32, (size, cell.shape[1]), 0)
    low, high = 1.0 - frac, frac
    inside = jnp.where(spots == cell, low, 0.0) + jnp.where(spots == cell + 1, high, 0.0)
    return inside, jnp.where(cell == -1, low, 0.0), jnp.where(cell == size - 1, high, 0.0)


def gather_rows(order_ref, section, source_ref, leave_ref, cap):
    def body(step, carry):
        for u in range(16):
            t = step * 16 + u
            leave_ref[section, pl.ds(t, 1), :] = source_ref[pl.ds(order_ref[section, t], 1), :]
        return carry

    lax.fori_loop(0, 8 * cap // 16, body, 0)


def build_onehot(slot_ref, section, onehot_ref):
    slot = slot_ref[section]
    moving = slot.shape[1]
    step_rows = 256

    def body(step, carry):
        base = pl.multiple_of(step * step_rows, step_rows)
        spots = lax.broadcasted_iota(jnp.int32, (step_rows, moving), 0) + base
        onehot_ref[pl.ds(base, step_rows), :] = jnp.where(spots == slot, 1.0, 0.0).astype(jnp.bfloat16)
        return carry

    lax.fori_loop(0, onehot_ref.shape[0] // step_rows, body, 0)


def build_plane(section, dims, v_ref, halo_ref, corner_ref, plane_ref):
    cx, cy = dims
    inner = cx * cy
    depth = v_ref.shape[3]
    for k in range(3):
        row = 3 * section + k
        own = v_ref[row].reshape(inner, depth)
        plane_ref[pl.ds(k * depth, depth), 0:inner] = own.T
        faces = halo_ref[row].astype(jnp.float32)
        corners = [corner_ref[d, row : row + 1, :] for d in range(4)]
        filler = jnp.zeros((128 - faces.shape[0] - 4, depth), jnp.float32)
        edge = jnp.concatenate([faces] + corners + [filler], axis=0)
        width = plane_ref.shape[1] - inner
        plane_ref[pl.ds(k * depth, depth), inner:] = edge.T[:, 0:width].astype(jnp.bfloat16)


def sample(section, dims, cells_ref, head_ref, plane_ref):
    cx, cy = dims
    depth = plane_ref.shape[0] // 3
    block = 256

    def body(step, carry):
        span = pl.ds(pl.multiple_of(step * block, block), block)
        head = head_ref[:, span]
        cell = cells_ref[section, :, span]
        wx, wx_low, wx_high = cell_weights(cx, cell[0:1], head[0:1])
        wy, wy_low, wy_high = cell_weights(cy, cell[1:2], head[1:2])
        wz, _, _ = cell_weights(depth, cell[2:3], head[2:3])
        parts = [wx[x : x + 1] * wy for x in range(cx)]
        parts += [wx_high * wy, wx_low * wy, wx * wy_high, wx * wy_low]
        parts += [wx_high * wy_high, wx_low * wy_low, wx_high * wy_low, wx_low * wy_high]
        parts += [jnp.zeros((12, block), jnp.float32)]
        whole = jnp.concatenate(parts, axis=0)
        high = whole.astype(jnp.bfloat16)
        low = (whole - high.astype(jnp.float32)).astype(jnp.bfloat16)
        columns = jnp.dot(plane_ref[...], high, preferred_element_type=jnp.float32)
        columns = columns + jnp.dot(plane_ref[...], low, preferred_element_type=jnp.float32)
        speed = jnp.concatenate(
            [
                jnp.sum(columns[k * depth : (k + 1) * depth] * wz, axis=0, keepdims=True)
                for k in range(3)
            ],
            axis=0,
        )
        moved = head[0:3] + GAMMA[section] * speed + ZETA[section] * head[3:6]
        head_ref[:, span] = jnp.concatenate([moved, speed, jnp.ones((2, block), jnp.float32)], axis=0)
        return carry

    lax.fori_loop(0, head_ref.shape[1] // block, body, 0)


def steps_kernel(
    sizes,
    cap,
    order_ref,
    slot_ref,
    taken_ref,
    cells_ref,
    v_ref,
    yface_ref,
    away_ref,
    state_ref,
    head_ref,
    arrived_ref,
    rows_ref,
    leave_ref,
    onehot_ref,
    plane_ref,
    halo_ref,
    corner_ref,
    head_out_ref,
    head_in_ref,
    send_sem,
    recv_sem,
):
    sems = (send_sem, recv_sem)
    sections = slot_ref.shape[0]
    cx, cy = v_ref.shape[1], v_ref.shape[2]
    count = state_ref.shape[0]
    moving = 8 * cap
    starts = (0, cy, 2 * cy, 2 * cy + cx)
    widths = (cy, cy, cx, cx)
    greet(sizes)

    halos = []
    for section in range(sections):
        group = []
        fields = pl.ds(3 * section, 3)
        for r in range(4):
            off_x, off_y = OFFSETS[r]
            src = v_ref.at[fields, cx - 1 if off_x > 0 else 0] if off_x else yface_ref.at[r - 2, fields]
            dst = halo_ref.at[fields, pl.ds(starts[r ^ 1], widths[r ^ 1]), :]
            group.append(send(r, src, dst, sems, section, sizes))
        if section == 0:
            for r in range(4, 8):
                group.append(send(r, away_ref.at[r - 4], corner_ref.at[(r ^ 1) - 4], sems, section, sizes))
        halos.append(group)

    def send_rows(section):
        gather_rows(order_ref, section, rows_ref, leave_ref, cap)
        return [
            send(
                r,
                leave_ref.at[section, pl.ds(r * cap, cap)],
                arrived_ref.at[pl.ds(section * moving + (r ^ 1) * cap, cap)],
                sems,
                sections + section,
                sizes,
            )
            for r in range(8)
        ]

    rows_ref[0:count, :] = state_ref[...]
    carried = send_rows(0)
    for b in range(count // 128):
        head_ref[:, b * 128 : (b + 1) * 128] = state_ref[b * 128 : (b + 1) * 128, :].T[0:8]
    for section in range(sections):
        if section == 0:
            build_onehot(slot_ref, 0, onehot_ref.at[0])
        for copy in halos[section]:
            copy.wait()
        build_plane(section, (cx, cy), v_ref, halo_ref, corner_ref, plane_ref)
        sample(section, (cx, cy), cells_ref, head_ref, plane_ref)
        hot = onehot_ref.at[section % 2]
        stacked = jnp.concatenate([part.astype(jnp.float32) for part in parts_of(head_ref[...])], axis=0)
        picked = jnp.dot(stacked.astype(jnp.bfloat16), hot[...], preferred_element_type=jnp.float32)
        leaving = picked[0:8] + picked[8:16] + picked[16:24]
        heads = []
        for r in range(8):
            head_out_ref[section, r] = leaving[:, r * cap : (r + 1) * cap]
        for r in range(8):
            heads.append(
                send(
                    r,
                    head_out_ref.at[section, r],
                    head_in_ref.at[section, r ^ 1],
                    sems,
                    2 * sections + section,
                    sizes,
                )
            )
        for copy in carried:
            copy.wait()
        if section + 1 < sections:
            low = section * moving
            rows_ref[count + low : count + low + moving, :] = arrived_ref[low : low + moving, :]
            carried = send_rows(section + 1)
            build_onehot(slot_ref, section + 1, onehot_ref.at[(section + 1) % 2])
        for copy in heads:
            copy.wait()
        came = jnp.concatenate([head_in_ref[section, r] for r in range(8)], axis=1)
        came = came * taken_ref[section]
        stacked = jnp.concatenate([part.astype(jnp.float32) for part in parts_of(came)], axis=0)
        spread = lax.dot_general(
            stacked.astype(jnp.bfloat16), hot[...], (((1,), (1,)), ((), ())), preferred_element_type=jnp.float32
        )
        placed = spread[0:8] + spread[8:16] + spread[16:24]
        head_ref[...] = jnp.where(placed[6:7] > 0.5, placed, head_ref[...])


def last_kernel(goal_ref, state_ref, arrived_ref, head_ref, out_ref, rows_ref):
    count, width = out_ref.shape
    sections, moving = goal_ref.shape
    rows_ref[0:count, :] = state_ref[...]
    for section in range(sections):

        def body(step, carry):
            for u in range(16):
                t = step * 16 + u
                rows_ref[pl.ds(goal_ref[section, t], 1), :] = arrived_ref[pl.ds(section * moving + t, 1), :]
            return carry

        lax.fori_loop(0, moving // 16, body, 0)
    lanes = lax.broadcasted_iota(jnp.int32, (128, width), 1)
    for b in range(count // 128):
        span = slice(b * 128, (b + 1) * 128)
        full = jnp.concatenate([head_ref[:, span], jnp.zeros((width - 8, 128), jnp.float32)], axis=0)
        out_ref[span, :] = jnp.where(lanes < 6, full.T, rows_ref[span, :])


def local(sizes, cap, state, velocity, cells, slots, counts):
    sections, _, cx, cy, depth = velocity.shape
    count, width = state.shape
    moving = 8 * cap
    fields = sections * 3
    field = velocity.reshape(fields, cx, cy, depth)
    yface = jnp.stack([field[:, :, cy - 1, :], field[:, :, 0, :]])
    away = jnp.stack(
        [field[:, cx - 1, cy - 1], field[:, 0, 0], field[:, cx - 1, 0], field[:, 0, cy - 1]]
    ).astype(jnp.float32)
    away = jnp.pad(away, ((0, 0), (0, -fields % 8), (0, 0)))
    order = slots[:, 0:moving]
    limits = jnp.repeat(counts.reshape(sections, 8), cap, axis=1)
    within = jnp.tile(jnp.arange(cap, dtype=jnp.int32), 8)[None, :]
    taken = within < limits
    goal = jnp.where(taken, order, count)
    places = jnp.arange(moving, dtype=jnp.int32)[:, None]
    sources = [order[0]]
    for section in range(1, sections):
        found = jnp.full((moving,), -1, jnp.int32)
        for past in range(section):
            match = goal[past][:, None] == order[section][None, :]
            found = jnp.maximum(
                found, jnp.max(jnp.where(match, count + past * moving + places, -1), axis=0)
            )
        sources.append(jnp.where(found >= 0, found, order[section]))
    sources = jnp.stack(sources)

    head, arrived = pl.pallas_call(
        functools.partial(steps_kernel, sizes, cap),
        out_shape=(
            jax.ShapeDtypeStruct((8, count), jnp.float32),
            jax.ShapeDtypeStruct((sections * moving, width), jnp.float32),
        ),
        in_specs=[SMEM] + [VMEM] * 7,
        out_specs=(VMEM, VMEM),
        scratch_shapes=[
            pltpu.VMEM((count + (sections - 1) * moving, width), jnp.float32),
            pltpu.VMEM((sections, moving, width), jnp.float32),
            pltpu.VMEM((2, count, moving), jnp.bfloat16),
            pltpu.VMEM((3 * depth, cx * cy + 2 * cx + 2 * cy + 16), jnp.bfloat16),
            pltpu.VMEM((fields, 2 * cx + 2 * cy, depth), jnp.bfloat16),
            pltpu.VMEM(away.shape, jnp.float32),
            pltpu.VMEM((sections, 8, 8, cap), jnp.float32),
            pltpu.VMEM((sections, 8, 8, cap), jnp.float32),
            pltpu.SemaphoreType.DMA((3 * sections, 8)),
            pltpu.SemaphoreType.DMA((3 * sections, 8)),
        ],
        compiler_params=pltpu.CompilerParams(collective_id=0, has_side_effects=True),
    )(
        sources,
        order.reshape(sections, 1, moving),
        taken.astype(jnp.float32).reshape(sections, 1, moving),
        cells,
        field,
        yface,
        away,
        state,
    )
    return pl.pallas_call(
        last_kernel,
        out_shape=jax.ShapeDtypeStruct((count, width), jnp.float32),
        in_specs=[SMEM, VMEM, VMEM, VMEM],
        out_specs=VMEM,
        scratch_shapes=[pltpu.VMEM((count + SPARE, width), jnp.float32)],
    )(goal, state, arrived, head)


def solution(mesh):
    return jax.shard_map(
        functools.partial(local, (mesh.shape["gx"], mesh.shape["gy"]), 64),
        mesh=mesh,
        in_specs=(
            P(("gx", "gy"), None),
            P(None, None, "gx", "gy", None),
            P(None, None, ("gx", "gy")),
            P(None, ("gx", "gy")),
            P(None, "gx", "gy", None),
        ),
        out_specs=P(("gx", "gy"), None),
        check_vma=False,
    )
```

profile of v0, /device:TPU:1, one launch (start us, length us, event | category | flops | bytes accessed | tf_op | source)
XLA Modules:
  0.0 56.2 jit_solution(11575550908031608188)
XLA Ops:
  0.0 0.0 copy-start.1
  0.0 0.7 %copy-done.1 = s32[3,1,1,8]{3,2,1,0:T(1,128)S(1)} copy-done((s32[3,1,1,8]{3,2,1,0:T(1,128)S(1)}, s32[3,1,1,8]{3,2,1,0:T(1,128)}, u32[]{:S(2)}) %copy-start.1) | copy-done | bytes 120
  0.7 0.1 lt.23
  0.8 0.8 %fusion.11 = (s32[1,512]{1,0:T(1,128)S(1)}, s32[1,512]{1,0:T(1,128)S(1)}) fusion(s32[3,2048]{1,0:T(4,128)} %param.8), kind=kLoop, calls=%fused_computation.33 | loop fusion | bytes 8192 | tf_op jit(solution)/shard_map/slice | solution.py:285
  1.6 0.1 broadcast_in_dim.32
  1.6 0.1 reshape.113
  1.7 0.1 reshape.111
  1.8 0.6 %compare_convert_fusion.taken_ref = f32[3,1,512]{2,1,0:T(1,128)} fusion(s32[3,1,512]{2,1,0:T(1,128)S(1)} %reshape.113, s32[512]{0:T(512)S(1)} %lt.23), kind=kLoop, calls=%fused_computation.11 | loop fusion | flops 3072 | bytes 14336 | tf_op jit(solution)/shard_map/convert_element_type | solution.py:316
  2.4 0.7 %slice_bitcast_fusion = (s32[3,1,512]{2,0,1:T(4,128)S(1)}, s32[3,512]{1,0:T(4,128)S(1)}) fusion(s32[3,2048]{1,0:T(4,128)} %param.8, s32[3,512]{1,0:T(4,128)S(1)} %reshape.111, s32[512]{0:T(512)S(1)} %lt.23), kind=kLoop, calls=%fused_computation.20 | loop fusion | flops 3072 | bytes 26624 | tf_op jit(solution)/shard_map/reshape | solution.py:315
  3.1 0.0 copy-start
  3.1 0.6 %copy.24.slot_ref = s32[3,1,512]{2,1,0:T(1,128)} copy(s32[3,1,512]{2,0,1:T(4,128)S(1)} %get-tuple-element.18) | data formatting | bytes 12288 | tf_op jit(solution)/shard_map/reshape | solution.py:315
  3.7 0.0 copy-done
  3.7 0.6 %select_reduce_fusion.2 = (s32[512]{0:T(512)S(1)}, s32[512]{0:T(512)S(1)}, s32[512]{0:T(512)S(1)}) fusion(s32[512]{0:T(512)S(1)} %iota_add_fusion.1, s32[512]{0:T(512)S(1)} %bitcast.29, s32[512]{0:T(512)S(1)} %bitcast.31, s32[512]{0:T(512)S(1)} %bitcast.28, s32[512]{0:T(512)S(1)} %iota_add_fusion, s32[512]{0:T(512)S(1)} %bitcast.30), kind=kLoop, calls=%fused_computation.2 | loop fusion | flops 2357760 | bytes 18432 | tf_op jit(solution)/shard_map/reduce_max | solution.py:287
  4.3 0.8 %fusion.10 = (s32[1,512]{1,0:T(1,128)S(1)}, s32[1,512]{1,0:T(1,128)S(1)}, s32[1,512]{1,0:T(1,128)S(1)}) fusion(s32[3,2048]{1,0:T(4,128)} %param.8, s32[1,512]{1,0:T(1,128)S(1)} %bitcast.33, s32[1,512]{1,0:T(1,128)S(1)} %bitcast.32), kind=kLoop, calls=%fused_computation.32 | loop fusion | flops 2048 | bytes 16384 | tf_op jit(solution)/shard_map/slice | solution.py:281
  5.2 0.6 %pad_add_fusion.order_ref = s32[3,512]{1,0:T(4,128)} fusion(s32[1,512]{1,0:T(1,128)S(1)} %get-tuple-element.22, s32[1,512]{1,0:T(1,128)S(1)} %get-tuple-element.21, s32[1,512]{1,0:T(1,128)S(1)} %get-tuple-element.20), kind=kLoop, calls=%fused_computation.18 | loop fusion | flops 3072 | bytes 12288 | tf_op jit(solution)/shard_map/stack | solution.py:290
  5.8 0.8 %fusion.8 = (bf16[9,1,1,128]{3,2,1,0:T(2,128)(2,1)S(1)}, bf16[9,1,1,128]{3,2,1,0:T(2,128)(2,1)S(1)}, bf16[9,1,1,128]{3,2,1,0:T(2,128)(2,1)S(1)}, bf16[9,1,1,128]{3,2,1,0:T(2,128)(2,1)S(1)}) fusion(bf16[9,16,16,128]{3,2,1,0:T(8,128)(2,1)} %bitcast.24), kind=kLoop, calls=%fused_computation.30 | loop fusion | bytes 18432 | tf_op jit(solution)/shard_map/slice | solution.py:272
  6.6 0.6 %fusion.7.away_ref = f32[4,16,128]{2,1,0:T(8,128)} fusion(bf16[1,9,128]{2,1,0:T(8,128)(2,1)S(1)} %get-tuple-element.31, bf16[1,9,128]{2,1,0:T(8,128)(2,1)S(1)} %get-tuple-element.32, bf16[1,9,128]{2,1,0:T(8,128)(2,1)S(1)} %get-tuple-element.33, bf16[1,9,128]{2,1,0:T(8,128)(2,1)S(1)} %get-tuple-element.34), kind=kLoop, calls=%fused_computation.15 | loop fusion | flops 106496 | bytes 41984 | tf_op jit(solution)/shard_map/jit(_pad)/pad | solution.py:274
  7.2 1.2 %fusion.9 = (bf16[9,16,1,128]{3,2,1,0:T(2,128)(2,1)S(1)}, bf16[9,16,1,128]{3,2,1,0:T(2,128)(2,1)S(1)}) fusion(bf16[9,16,16,128]{3,2,1,0:T(8,128)(2,1)} %bitcast.25), kind=kLoop, calls=%fused_computation.31 | loop fusion | bytes 147456 | tf_op jit(solution)/shard_map/slice | solution.py:270
  8.4 0.6 %pad_maximum_fusion.yface_ref = bf16[2,9,16,128]{3,2,1,0:T(8,128)(2,1)} fusion(bf16[1,9,16,128]{3,2,1,0:T(8,128)(2,1)S(1)} %get-tuple-element.29, bf16[1,9,16,128]{3,2,1,0:T(8,128)(2,1)S(1)} %get-tuple-element.30), kind=kLoop, calls=%fused_computation.3 | loop fusion | flops 36864 | bytes 147456 | tf_op jit(solution)/shard_map/stack | solution.py:270
  9.0 40.8 %shard_map.55 = (f32[8,2048]{1,0:T(8,128)}, f32[1536,128]{1,0:T(8,128)}) custom-call(s32[3,512]{1,0:T(4,128)} %pad_add_fusion.order_ref, s32[3,1,512]{2,1,0:T(1,128)} %copy.24.slot_ref, f32[3,1,512]{2,1,0:T(1,128)} %compare_convert_fusion.taken_ref, s32[3,3,2048]{2,1,0:T(4,128)} %cells_ref.1, bf16[9,16,16,128]{3,2,1,0:T(8,128)(2,1)} %bitcast.26, ...), custom_call_target="tpu_custom_call" | custom-call | tf_op jit(solution)/shard_map/pallas_call | solution.py:292
  49.8 6.4 %shard_map.56 = f32[2048,128]{1,0:T(8,128)} custom-call(s32[3,512]{1,0:T(4,128)} %copy-done, f32[2048,128]{1,0:T(8,128)} %state_ref.3, f32[1536,128]{1,0:T(8,128)} %get-tuple-element.7.arrived_ref, f32[8,2048]{1,0:T(8,128)} %get-tuple-element.8.head_ref), custom_call_target="tpu_custom_call" | custom-call | tf_op jit(solution)/shard_map/pallas_call | solution.py:323
  (9 shorter events, 0.0 us)
Async XLA Ops:
  0.0 0.7 %copy-start.1 = (s32[3,1,1,8]{3,2,1,0:T(1,128)S(1)}, s32[3,1,1,8]{3,2,1,0:T(1,128)}, u32[]{:S(2)}) copy-start(s32[3,1,1,8]{3,2,1,0:T(1,128)} %param.9) | copy-start | bytes 292
  3.1 0.6 %copy-start = (s32[3,512]{1,0:T(4,128)}, s32[3,512]{1,0:T(4,128)S(1)}, u32[]{:S(2)}) copy-start(s32[3,512]{1,0:T(4,128)S(1)} %get-tuple-element.19.goal_ref) | copy-start | bytes 18436
where the time goes:
time: 56.7 us; the launch traced here: 56.2 us
  Pallas kernels  47.2 us (83%)
  other arithmetic  4.61 us (8%)
  local copies, waits for them, and re-layouts  4.36 us (8%)
    pallas_call x1, Pallas kernels, local(): pl.pallas_call(functools.partial(steps_kernel, sizes, cap), out_shape=(ja...  40.8 us
    pallas_call x1, Pallas kernels, local(): pl.pallas_call(last_kernel, out_shape=jax.ShapeDtypeStruct((count, width)...  6.39 us
    slice x1, local copies, waits for them, and re-layouts, local(): yface = jnp.stack([field[:, :, cy - 1, :], field[:, :, 0, :]])  1.17 us

commit v1 on v0

--- a/solution.py
+++ b/solution.py
@@ -58,10 +58,12 @@
 
 
 def gather_rows(order_ref, section, source_ref, leave_ref, cap):
+    first = section * 8 * cap
+
     def body(step, carry):
         for u in range(16):
             t = step * 16 + u
-            leave_ref[section, pl.ds(t, 1), :] = source_ref[pl.ds(order_ref[section, t], 1), :]
+            leave_ref[section, pl.ds(t, 1), :] = source_ref[pl.ds(order_ref[first + t], 1), :]
         return carry
 
     lax.fori_loop(0, 8 * cap // 16, body, 0)
@@ -130,6 +132,55 @@
         return carry
 
     lax.fori_loop(0, head_ref.shape[1] // block, body, 0)
+
+
+def plan_kernel(cap, slots_ref, counts_ref, v_ref, index_ref, slot_ref, taken_ref, yface_ref, away_ref):
+    sections, count = slots_ref.shape
+    moving = 8 * cap
+    fields, inner, depth = v_ref.shape
+    cx = yface_ref.shape[2]
+    cy = inner // cx
+    lanes = lax.broadcasted_iota(jnp.int32, (1, moving), 1)
+    within = lax.rem(lanes, cap)
+    places = lax.broadcasted_iota(jnp.int32, (moving, moving), 0) + count
+    chunks = moving // 128
+    columns = []
+    for section in range(sections):
+        slot = slots_ref[section : section + 1, 0:moving]
+        limit = jnp.zeros((1, moving), jnp.int32)
+        for r in range(8):
+            limit = jnp.where(lanes >= r * cap, counts_ref[section, r], limit)
+        taken = within < limit
+        goal = jnp.where(taken, slot, count)
+        found = jnp.full((1, moving), -1, jnp.int32)
+        for past in range(section):
+            match = columns[past] == slot
+            best = jnp.max(jnp.where(match, places, -1), axis=0, keepdims=True)
+            found = jnp.where(best >= 0, best + past * moving, found)
+        source = jnp.where(found >= 0, found, slot)
+        if section + 1 < sections:
+            wide = jnp.broadcast_to(goal.astype(jnp.float32), (8, moving))
+            columns.append(wide.T[:, 0:1].astype(jnp.int32))
+        slot_ref[section] = slot
+        taken_ref[section] = jnp.where(taken, 1.0, 0.0)
+        for c in range(chunks):
+            span = slice(c * 128, (c + 1) * 128)
+            row = section * chunks + c
+            index_ref[row : row + 1, :] = source[:, span]
+            row += sections * chunks
+            index_ref[row : row + 1, :] = goal[:, span]
+    row = lax.broadcasted_iota(jnp.int32, (2 * cx + 8, inner), 0)
+    place = lax.broadcasted_iota(jnp.int32, (2 * cx + 8, inner), 1)
+    want = jnp.where(row < cx, row * cy + cy - 1, (row - cx) * cy)
+    for d, spot in enumerate((inner - 1, 0, (cx - 1) * cy, cy - 1)):
+        want = jnp.where(row == 2 * cx + d, spot, want)
+    pick = jnp.where(want == place, 1.0, 0.0).astype(jnp.bfloat16)
+    for f in range(fields):
+        edge = jnp.dot(pick, v_ref[f], preferred_element_type=jnp.float32)
+        yface_ref[0, f] = edge[0:cx].astype(jnp.bfloat16)
+        yface_ref[1, f] = edge[cx : 2 * cx].astype(jnp.bfloat16)
+        for d in range(4):
+            away_ref[d, f : f + 1, :] = edge[2 * cx + d : 2 * cx + d + 1]
 
 
 def steps_kernel(
@@ -241,19 +292,17 @@
         head_ref[...] = jnp.where(placed[6:7] > 0.5, placed, head_ref[...])
 
 
-def last_kernel(goal_ref, state_ref, arrived_ref, head_ref, out_ref, rows_ref):
+def last_kernel(offset, index_ref, state_ref, arrived_ref, head_ref, out_ref, rows_ref):
     count, width = out_ref.shape
-    sections, moving = goal_ref.shape
     rows_ref[0:count, :] = state_ref[...]
-    for section in range(sections):
-
-        def body(step, carry):
-            for u in range(16):
-                t = step * 16 + u
-                rows_ref[pl.ds(goal_ref[section, t], 1), :] = arrived_ref[pl.ds(section * moving + t, 1), :]
-            return carry
-
-        lax.fori_loop(0, moving // 16, body, 0)
+
+    def body(step, carry):
+        for u in range(16):
+            t = step * 16 + u
+            rows_ref[pl.ds(index_ref[offset + t], 1), :] = arrived_ref[pl.ds(t, 1), :]
+        return carry
+
+    lax.fori_loop(0, arrived_ref.shape[0] // 16, body, 0)
     lanes = lax.broadcasted_iota(jnp.int32, (128, width), 1)
     for b in range(count // 128):
         span = slice(b * 128, (b + 1) * 128)
@@ -267,27 +316,22 @@
     moving = 8 * cap
     fields = sections * 3
     field = velocity.reshape(fields, cx, cy, depth)
-    yface = jnp.stack([field[:, :, cy - 1, :], field[:, :, 0, :]])
-    away = jnp.stack(
-        [field[:, cx - 1, cy - 1], field[:, 0, 0], field[:, cx - 1, 0], field[:, 0, cy - 1]]
-    ).astype(jnp.float32)
-    away = jnp.pad(away, ((0, 0), (0, -fields % 8), (0, 0)))
-    order = slots[:, 0:moving]
-    limits = jnp.repeat(counts.reshape(sections, 8), cap, axis=1)
-    within = jnp.tile(jnp.arange(cap, dtype=jnp.int32), 8)[None, :]
-    taken = within < limits
-    goal = jnp.where(taken, order, count)
-    places = jnp.arange(moving, dtype=jnp.int32)[:, None]
-    sources = [order[0]]
-    for section in range(1, sections):
-        found = jnp.full((moving,), -1, jnp.int32)
-        for past in range(section):
-            match = goal[past][:, None] == order[section][None, :]
-            found = jnp.maximum(
-                found, jnp.max(jnp.where(match, count + past * moving + places, -1), axis=0)
-            )
-        sources.append(jnp.where(found >= 0, found, order[section]))
-    sources = jnp.stack(sources)
+    rows = 2 * sections * moving // 128
+    rows += -rows % 8
+    edges = (4, fields + -fields % 8, depth)
+    index, slot, taken, yface, away = pl.pallas_call(
+        functools.partial(plan_kernel, cap),
+        out_shape=(
+            jax.ShapeDtypeStruct((rows, 128), jnp.int32),
+            jax.ShapeDtypeStruct((sections, 1, moving), jnp.int32),
+            jax.ShapeDtypeStruct((sections, 1, moving), jnp.float32),
+            jax.ShapeDtypeStruct((2, fields, cx, depth), field.dtype),
+            jax.ShapeDtypeStruct(edges, jnp.float32),
+        ),
+        in_specs=[VMEM, SMEM, VMEM],
+        out_specs=(VMEM,) * 5,
+    )(slots, counts.reshape(sections, 8), field.reshape(fields, cx * cy, depth))
+    index = index.reshape(rows * 128)
 
     head, arrived = pl.pallas_call(
         functools.partial(steps_kernel, sizes, cap),
@@ -303,7 +347,7 @@
             pltpu.VMEM((2, count, moving), jnp.bfloat16),
             pltpu.VMEM((3 * depth, cx * cy + 2 * cx + 2 * cy + 16), jnp.bfloat16),
             pltpu.VMEM((fields, 2 * cx + 2 * cy, depth), jnp.bfloat16),
-            pltpu.VMEM(away.shape, jnp.float32),
+            pltpu.VMEM(edges, jnp.float32),
             pltpu.VMEM((sections, 8, 8, cap), jnp.float32),
             pltpu.VMEM((sections, 8, 8, cap), jnp.float32),
             pltpu.SemaphoreType.DMA((3 * sections, 8)),
@@ -311,9 +355,9 @@
         ],
         compiler_params=pltpu.CompilerParams(collective_id=0, has_side_effects=True),
     )(
-        sources,
-        order.reshape(sections, 1, moving),
-        taken.astype(jnp.float32).reshape(sections, 1, moving),
+        index,
+        slot,
+        taken,
         cells,
         field,
         yface,
@@ -321,12 +365,12 @@
         state,
     )
     return pl.pallas_call(
-        last_kernel,
+        functools.partial(last_kernel, sections * moving),
         out_shape=jax.ShapeDtypeStruct((count, width), jnp.float32),
         in_specs=[SMEM, VMEM, VMEM, VMEM],
         out_specs=VMEM,
         scratch_shapes=[pltpu.VMEM((count + SPARE, width), jnp.float32)],
-    )(goal, state, arrived, head)
+    )(index, state, arrived, head)
 
 
 def solution(mesh):

time: 56.7 us -> 49.7 us (0.88)
  other arithmetic: 4.61 us -> 0 us
  local copies, waits for them, and re-layouts: 4.36 us -> 1.25 us
  Pallas kernels: 47.2 us -> 48.2 us
    slice x4 -> x0, local copies, waits for them, and re-layouts: 2.74 us -> none  [the longest x1 1.17 us: local(): yface = jnp.stack([field[:, :, cy - 1, :], field[:, :, 0, :]])]
    another operation x2 -> x0, other arithmetic: 1.25 us -> none  [the longest x1 0.64 us: local(): yface = jnp.stack([field[:, :, cy - 1, :], field[:, :, 0, :]])]
    slice x1 -> x0, other arithmetic: 0.82 us -> none  [local(): sources = [order[0]]]
    reshape x3 -> x0, local copies, waits for them, and re-layouts: 0.76 us -> none  [the longest x1 0.6 us: local(): order.reshape(sections, 1, moving)]
    reshape x1 -> x0, other arithmetic: 0.7 us -> none  [local(): order.reshape(sections, 1, moving)]
    pallas_call x1 -> x2, Pallas kernels: 6.39 us -> 7.05 us  [the longest x1 4.52 us: local(): pl.pallas_call(functools.partial(last_kernel, sections * moving), out_sha...]
    reduce_max x1 -> x0, other arithmetic: 0.61 us -> none  [local(): jnp.max(jnp.where(match, count + past * moving + places, -1), axis=0)]
    pad x1 -> x0, other arithmetic: 0.61 us -> none  [local(): away = jnp.pad(away, ((0, 0), (0, -fields % 8), (0, 0)))]
where the time goes in v1:
time: 49.7 us; the launch traced here: 49.5 us
  Pallas kernels  48.2 us (97%)
  local copies, waits for them, and re-layouts  1.25 us (3%)
    pallas_call x1, Pallas kernels, local(): pl.pallas_call(functools.partial(steps_kernel, sizes, cap), out_shape=(ja...  41.2 us
    pallas_call x1, Pallas kernels, local(): pl.pallas_call(functools.partial(last_kernel, sections * moving), out_sha...  4.52 us
    pallas_call x1, Pallas kernels, local(): pl.pallas_call(functools.partial(plan_kernel, cap), out_shape=(jax.ShapeD...  2.53 us
    unnamed x3, local copies, waits for them, and re-layouts  1.25 us

profile of v1, /device:TPU:1, one launch (start us, length us, event | category | flops | bytes accessed | tf_op | source)
XLA Modules:
  0.0 49.5 jit_solution(7580608127311430878)
XLA Ops:
  0.0 0.0 copy-start
  0.0 0.7 %copy-done = s32[3,1,1,8]{3,2,1,0:T(1,128)S(1)} copy-done((s32[3,1,1,8]{3,2,1,0:T(1,128)S(1)}, s32[3,1,1,8]{3,2,1,0:T(1,128)}, u32[]{:S(2)}) %copy-start) | copy-done | bytes 120
  0.7 0.6 %copy.8 = s32[3,1,1,8]{3,0,1,2:T(4,128)} copy(s32[3,1,1,8]{3,2,1,0:T(1,128)S(1)} %copy-done) | data formatting | bytes 192
  1.3 2.5 %shard_map.55 = (s32[24,128]{1,0:T(8,128)}, s32[3,1,512]{2,1,0:T(1,128)}, f32[3,1,512]{2,1,0:T(1,128)}, bf16[2,9,16,128]{3,2,1,0:T(8,128)(2,1)}, f32[4,16,128]{2,1,0:T(8,128)}) custom-call(s32[3,2048]{1,0:T(4,128)} %slots_ref.1, s32[3,8]{1,0:T(4,128)} %bitcast.10, bf16[9,256,128]{2,1,0:T(8,128)(2,1)} %bitcast.6), custom_call_target="tpu_custom_call" | custom-call | tf_op jit(solution)/shard_map/pallas_call | solution.py:322
  3.8 41.2 %shard_map.56 = (f32[8,2048]{1,0:T(8,128)}, f32[1536,128]{1,0:T(8,128)}) custom-call(s32[3072]{0:T(1024)} %bitcast.8, s32[3,1,512]{2,1,0:T(1,128)} %get-tuple-element.13.slot_ref, f32[3,1,512]{2,1,0:T(1,128)} %get-tuple-element.14.taken_ref, s32[3,3,2048]{2,1,0:T(4,128)} %cells_ref.1, bf16[9,16,16,128]{3,2,1,0:T(8,128)(2,1)} %bitcast.7, ...), custom_call_target="tpu_custom_call" | custom-call | tf_op jit(solution)/shard_map/pallas_call | solution.py:336
  45.0 4.5 %shard_map.57 = f32[2048,128]{1,0:T(8,128)} custom-call(s32[3072]{0:T(1024)} %bitcast.9, f32[2048,128]{1,0:T(8,128)} %state_ref.3, f32[1536,128]{1,0:T(8,128)} %get-tuple-element.17.arrived_ref, f32[8,2048]{1,0:T(8,128)} %get-tuple-element.18.head_ref), custom_call_target="tpu_custom_call" | custom-call | tf_op jit(solution)/shard_map/pallas_call | solution.py:367
Async XLA Ops:
  0.0 0.7 %copy-start = (s32[3,1,1,8]{3,2,1,0:T(1,128)S(1)}, s32[3,1,1,8]{3,2,1,0:T(1,128)}, u32[]{:S(2)}) copy-start(s32[3,1,1,8]{3,2,1,0:T(1,128)} %param.9) | copy-start | bytes 292

commit v2 on v1

--- a/solution.py
+++ b/solution.py
@@ -11,6 +11,7 @@
 ZETA = (0.0, -17.0 / 60.0, -5.0 / 12.0)
 OFFSETS = ((1, 0), (-1, 0), (0, 1), (0, -1), (1, 1), (-1, -1), (1, -1), (-1, 1))
 SPARE = 8
+BLOCK = 512
 MESH = pl.DeviceIdType.MESH
 VMEM = pl.BlockSpec(memory_space=pltpu.VMEM)
 SMEM = pl.BlockSpec(memory_space=pltpu.SMEM)
@@ -99,36 +100,36 @@
         plane_ref[pl.ds(k * depth, depth), inner:] = edge.T[:, 0:width].astype(jnp.bfloat16)
 
 
-def sample(section, dims, cells_ref, head_ref, plane_ref):
+def sample(section, dims, head, cell, plane_ref):
     cx, cy = dims
     depth = plane_ref.shape[0] // 3
-    block = 256
+    block = head.shape[1]
+    wx, wx_low, wx_high = cell_weights(cx, cell[0:1], head[0:1])
+    wy, wy_low, wy_high = cell_weights(cy, cell[1:2], head[1:2])
+    wz, _, _ = cell_weights(depth, cell[2:3], head[2:3])
+    parts = [wx[x : x + 1] * wy for x in range(cx)]
+    parts += [wx_high * wy, wx_low * wy, wx * wy_high, wx * wy_low]
+    parts += [wx_high * wy_high, wx_low * wy_low, wx_high * wy_low, wx_low * wy_high]
+    parts += [jnp.zeros((12, block), jnp.float32)]
+    whole = jnp.concatenate(parts, axis=0)
+    high = whole.astype(jnp.bfloat16)
+    low = (whole - high.astype(jnp.float32)).astype(jnp.bfloat16)
+    columns = jnp.dot(plane_ref[...], high, preferred_element_type=jnp.float32)
+    columns = columns + jnp.dot(plane_ref[...], low, preferred_element_type=jnp.float32)
+    speed = jnp.concatenate(
+        [jnp.sum(columns[k * depth : (k + 1) * depth] * wz, axis=0, keepdims=True) for k in range(3)],
+        axis=0,
+    )
+    moved = head[0:3] + GAMMA[section] * speed + ZETA[section] * head[3:6]
+    return jnp.concatenate([moved, speed, jnp.ones((2, block), jnp.float32)], axis=0)
+
+
+def sample_all(section, dims, cells_ref, head_ref, plane_ref):
+    block = BLOCK
 
     def body(step, carry):
         span = pl.ds(pl.multiple_of(step * block, block), block)
-        head = head_ref[:, span]
-        cell = cells_ref[section, :, span]
-        wx, wx_low, wx_high = cell_weights(cx, cell[0:1], head[0:1])
-        wy, wy_low, wy_high = cell_weights(cy, cell[1:2], head[1:2])
-        wz, _, _ = cell_weights(depth, cell[2:3], head[2:3])
-        parts = [wx[x : x + 1] * wy for x in range(cx)]
-        parts += [wx_high * wy, wx_low * wy, wx * wy_high, wx * wy_low]
-        parts += [wx_high * wy_high, wx_low * wy_low, wx_high * wy_low, wx_low * wy_high]
-        parts += [jnp.zeros((12, block), jnp.float32)]
-        whole = jnp.concatenate(parts, axis=0)
-        high = whole.astype(jnp.bfloat16)
-        low = (whole - high.astype(jnp.float32)).astype(jnp.bfloat16)
-        columns = jnp.dot(plane_ref[...], high, preferred_element_type=jnp.float32)
-        columns = columns + jnp.dot(plane_ref[...], low, preferred_element_type=jnp.float32)
-        speed = jnp.concatenate(
-            [
-                jnp.sum(columns[k * depth : (k + 1) * depth] * wz, axis=0, keepdims=True)
-                for k in range(3)
-            ],
-            axis=0,
-        )
-        moved = head[0:3] + GAMMA[section] * speed + ZETA[section] * head[3:6]
-        head_ref[:, span] = jnp.concatenate([moved, speed, jnp.ones((2, block), jnp.float32)], axis=0)
+        head_ref[:, span] = sample(section, dims, head_ref[:, span], cells_ref[section, :, span], plane_ref)
         return carry
 
     lax.fori_loop(0, head_ref.shape[1] // block, body, 0)
@@ -149,7 +150,7 @@
         slot = slots_ref[section : section + 1, 0:moving]
         limit = jnp.zeros((1, moving), jnp.int32)
         for r in range(8):
-            limit = jnp.where(lanes >= r * cap, counts_ref[section, r], limit)
+            limit = jnp.where(lanes >= r * cap, counts_ref[section, 0, 0, r], limit)
         taken = within < limit
         goal = jnp.where(taken, slot, count)
         found = jnp.full((1, moving), -1, jnp.int32)
@@ -251,14 +252,23 @@
     for section in range(sections):
         if section == 0:
             build_onehot(slot_ref, 0, onehot_ref.at[0])
+        hot = onehot_ref.at[section % 2]
+        where_ = cells_ref[section].astype(jnp.float32)
+        stacked = [part.astype(jnp.float32) for part in parts_of(head_ref[...])] + [where_]
+        stacked = jnp.concatenate(stacked, axis=0).astype(jnp.bfloat16)
+        picked = jnp.dot(stacked, hot[...], preferred_element_type=jnp.float32)
+        leaving = picked[0:8] + picked[8:16] + picked[16:24]
+        there = picked[24:27].astype(jnp.int32)
         for copy in halos[section]:
             copy.wait()
         build_plane(section, (cx, cy), v_ref, halo_ref, corner_ref, plane_ref)
-        sample(section, (cx, cy), cells_ref, head_ref, plane_ref)
-        hot = onehot_ref.at[section % 2]
-        stacked = jnp.concatenate([part.astype(jnp.float32) for part in parts_of(head_ref[...])], axis=0)
-        picked = jnp.dot(stacked.astype(jnp.bfloat16), hot[...], preferred_element_type=jnp.float32)
-        leaving = picked[0:8] + picked[8:16] + picked[16:24]
+        leaving = jnp.concatenate(
+            [
+                sample(section, (cx, cy), leaving[:, b : b + BLOCK], there[:, b : b + BLOCK], plane_ref)
+                for b in range(0, moving, BLOCK)
+            ],
+            axis=1,
+        )
         heads = []
         for r in range(8):
             head_out_ref[section, r] = leaving[:, r * cap : (r + 1) * cap]
@@ -273,6 +283,7 @@
                     sizes,
                 )
             )
+        sample_all(section, (cx, cy), cells_ref, head_ref, plane_ref)
         for copy in carried:
             copy.wait()
         if section + 1 < sections:
@@ -330,7 +341,7 @@
         ),
         in_specs=[VMEM, SMEM, VMEM],
         out_specs=(VMEM,) * 5,
-    )(slots, counts.reshape(sections, 8), field.reshape(fields, cx * cy, depth))
+    )(slots, counts, field.reshape(fields, cx * cy, depth))
     index = index.reshape(rows * 128)
 
     head, arrived = pl.pallas_call(

time: 49.7 us -> 39.3 us (0.79)
  Pallas kernels: 48.2 us -> 39.1 us
  local copies, waits for them, and re-layouts: 1.25 us -> 0 us
    pallas_call x1, Pallas kernels: 41.2 us -> 32.1 us  [local(): pl.pallas_call(functools.partial(steps_kernel, sizes, cap), out_shape=(ja...]
    unnamed x3 -> x0, local copies, waits for them, and re-layouts: 1.25 us -> none
where the time goes in v2:
time: 39.3 us; the launch traced here: 39.1 us
  Pallas kernels  39.1 us (99%)
    pallas_call x1, Pallas kernels, local(): pl.pallas_call(functools.partial(steps_kernel, sizes, cap), out_shape=(ja...  32.1 us
    pallas_call x1, Pallas kernels, local(): pl.pallas_call(functools.partial(last_kernel, sections * moving), out_sha...  4.52 us
    pallas_call x1, Pallas kernels, local(): pl.pallas_call(functools.partial(plan_kernel, cap), out_shape=(jax.ShapeD...  2.53 us

profile of v2, /device:TPU:1, one launch (start us, length us, event | category | flops | bytes accessed | tf_op | source)
XLA Modules:
  0.0 39.1 jit_solution(10537660783445938965)
XLA Ops:
  0.0 2.5 %shard_map.55 = (s32[24,128]{1,0:T(8,128)}, s32[3,1,512]{2,1,0:T(1,128)}, f32[3,1,512]{2,1,0:T(1,128)}, bf16[2,9,16,128]{3,2,1,0:T(8,128)(2,1)}, f32[4,16,128]{2,1,0:T(8,128)}) custom-call(s32[3,2048]{1,0:T(4,128)} %slots_ref.1, s32[3,1,1,8]{3,2,1,0:T(1,128)} %counts_ref.1, bf16[9,256,128]{2,1,0:T(8,128)(2,1)} %bitcast.3), custom_call_target="tpu_custom_call" | custom-call | tf_op jit(solution)/shard_map/pallas_call | solution.py:333
  2.5 32.1 %shard_map.56 = (f32[8,2048]{1,0:T(8,128)}, f32[1536,128]{1,0:T(8,128)}) custom-call(s32[3072]{0:T(1024)} %bitcast.5, s32[3,1,512]{2,1,0:T(1,128)} %get-tuple-element.13.slot_ref, f32[3,1,512]{2,1,0:T(1,128)} %get-tuple-element.14.taken_ref, s32[3,3,2048]{2,1,0:T(4,128)} %cells_ref.1, bf16[9,16,16,128]{3,2,1,0:T(8,128)(2,1)} %bitcast.4, ...), custom_call_target="tpu_custom_call" | custom-call | tf_op jit(solution)/shard_map/pallas_call | solution.py:347
  34.6 4.5 %shard_map.57 = f32[2048,128]{1,0:T(8,128)} custom-call(s32[3072]{0:T(1024)} %bitcast.6, f32[2048,128]{1,0:T(8,128)} %state_ref.3, f32[1536,128]{1,0:T(8,128)} %get-tuple-element.17.arrived_ref, f32[8,2048]{1,0:T(8,128)} %get-tuple-element.18.head_ref), custom_call_target="tpu_custom_call" | custom-call | tf_op jit(solution)/shard_map/pallas_call | solution.py:378
